TPU v7x, 32 devices: a whole 2x2x4 slice. The times are simulated.
32 devices in a mesh: dp: 4 (over z), vocab: 8 (over y, x, core).
Axes of the slice: x: 2, y: 2, z: 4, core: 2. Of those that a mesh axis runs over, the one named last changes fastest.
Arguments:
- teacher_logits: bfloat16 [1536, 151552], P('dp', 'vocab'), may hold values from -40 to 320, as said below
- student_logits: bfloat16 [1536, 126976], P('dp', 'vocab'), may hold values from -40 to 320, as said below
- tile_dest: int32 [1184, 2], replicated, may hold values from 0 to 991, as said below
- tile_weight: bfloat16 [1184, 2, 128, 128], P('vocab'), may hold values from 0.0009994507 to 1
- token_mask: int32 [1536], P('dp'), may hold values from 0 to 1, as said below
Outputs:
- token_loss: float32 [1536], P('dp')
- mean_loss: float32 [], replicated
Inputs may be any that keep to these rules, and one draw needn't show every extreme that they name: `teacher_logits`: Real-valued logits. `student_logits`: Real-valued logits. `tile_dest`: row b names the student blocks of the 2 tiles of teacher block b. Student block s belongs to vocab index s // 124, teacher block b to vocab index b // 148. Of the tiles of the teacher blocks of one vocab index, at most 37 name student blocks of any one vocab index, and exactly 37 do for some vocab index. `token_mask`: at least one token has a 1.
All inputs are finite; a program needn't handle non-finite values.
Results may differ from a plain program's by a relative error of at most 0.0031.
Values may be sent and summed in bfloat16 or wider, within the bound.
A program may use at most 192 MiB of HBM per device.

v0:
```python
import jax
import jax.numpy as jnp
from jax import lax
from jax.sharding import PartitionSpec as P

BLOCK = 128
VS = 126976
K = 2


SMOOTH = 0.1


def teacher_norm(values):
    maximum = lax.pmax(jnp.max(values, axis=1), "vocab")
    totals = lax.psum(jnp.sum(jnp.exp(values - maximum[:, None]), axis=1), "vocab")
    return (maximum, totals)


def student_norm(values):
    maximum = lax.pmax(jnp.max(values, axis=1), "vocab")
    totals = lax.psum(jnp.sum(jnp.exp(values - maximum[:, None]), axis=1), "vocab")
    return (maximum, totals)


def routing(tile_dest, group_size, sb_dev):
    flat_dest = tile_dest.reshape(group_size, -1)
    owners = flat_dest // sb_dev
    local_block = flat_dest % sb_dev
    owner_hits = (owners[:, :, None] == jnp.arange(group_size, dtype=jnp.int32)).astype(jnp.int32)
    earlier = jnp.cumsum(owner_hits, axis=1) - owner_hits
    slot_rank = jnp.sum(owner_hits * earlier, axis=2)
    return (owners, local_block, slot_rank)


def local(teacher_logits, student_logits, tile_dest, tile_weight, token_mask):
    group_size = lax.axis_size("vocab")
    my_index = lax.axis_index("vocab")
    tok_rows = teacher_logits.shape[0]
    tb_dev = teacher_logits.shape[1] // BLOCK
    sb_dev = student_logits.shape[1] // BLOCK
    tile_count = tb_dev * K
    capacity = (tile_count + group_size - 1) // group_size
    teacher_vals = teacher_logits.astype(jnp.float32)
    teacher_max, teacher_sum = teacher_norm(teacher_vals)
    teacher_prob = (jnp.exp(teacher_vals - teacher_max[:, None]) / teacher_sum[:, None]).astype(
        jnp.bfloat16
    )
    prob_blocks = teacher_prob.reshape(tok_rows, tb_dev, BLOCK)
    weights = tile_weight.astype(jnp.float32)
    mapping = (weights / jnp.sum(weights, axis=(1, 3), keepdims=True)).astype(jnp.bfloat16)
    owners, local_block, slot_rank = routing(tile_dest, group_size, sb_dev)
    my_owner = lax.dynamic_index_in_dim(owners, my_index, 0, keepdims=False)
    my_rank = lax.dynamic_index_in_dim(slot_rank, my_index, 0, keepdims=False)
    my_slot = my_owner * capacity + my_rank
    placement = (
        jnp.arange(group_size * capacity, dtype=jnp.int32)[:, None] == my_slot[None, :]
    ).astype(jnp.bfloat16)
    mine = owners == my_index
    slot_hit = (
        (slot_rank[:, :, None] == jnp.arange(capacity, dtype=jnp.int32)) & mine[:, :, None]
    ).astype(jnp.float32)
    block_hit = (local_block[:, :, None] == jnp.arange(sb_dev, dtype=jnp.int32)).astype(jnp.float32)
    slot_table = (
        jnp.einsum("ric,rij->rcj", slot_hit, block_hit)
        .reshape(group_size * capacity, sb_dev)
        .astype(jnp.bfloat16)
    )
    partial_value = jnp.einsum(
        "tbc,bkcd->bktd", prob_blocks, mapping, preferred_element_type=jnp.float32
    )
    partial_value = partial_value.astype(jnp.bfloat16).reshape(tile_count, tok_rows, BLOCK)
    outgoing = jnp.einsum(
        "si,itd->std", placement, partial_value, preferred_element_type=jnp.float32
    )
    outgoing = outgoing.astype(jnp.bfloat16).reshape(group_size, capacity, tok_rows, BLOCK)
    received = lax.all_to_all(outgoing, "vocab", split_axis=0, concat_axis=0, tiled=True)
    item_count = received.shape[2]
    flat_items = received.reshape(group_size * capacity, item_count, BLOCK)
    summed = jnp.einsum("snd,sj->njd", flat_items, slot_table, preferred_element_type=jnp.float32)
    mapped = summed.reshape(item_count, sb_dev * BLOCK)
    target = (1.0 - SMOOTH) * mapped + SMOOTH / VS
    student_vals = student_logits.astype(jnp.float32)
    student_max, student_sum = student_norm(student_vals)
    student_logp = student_vals - student_max[:, None] - jnp.log(student_sum)[:, None]
    kl_part = jnp.sum(target * (jnp.log(target) - student_logp), axis=1)
    token_kl = lax.psum(kl_part, "vocab")
    mask_vals = token_mask.astype(jnp.float32)
    token_loss = mask_vals * token_kl
    loss_total, mask_total = lax.psum((jnp.sum(token_loss), jnp.sum(mask_vals)), "dp")
    return (token_loss, loss_total / mask_total)


def solution(mesh):
    in_specs = (P("dp", "vocab"), P("dp", "vocab"), P(), P("vocab", None, None, None), P("dp"))
    out_specs = (P("dp"), P())
    return jax.shard_map(local, mesh=mesh, in_specs=in_specs, out_specs=out_specs, check_vma=False)
```

profile of v0, /device:TPU:0, one launch (start us, length us, event | category | flops | bytes accessed | tf_op | source)
XLA Modules:
  0.0 689.5 jit_solution(376746244504882365)
XLA Ops:
  1.4 0.7 broadcast_remainder_fusion
  2.1 16.5 %copy.35 = bf16[384,15872]{0,1:T(8,128)(2,1)} copy(bf16[384,15872]{1,0:T(8,128)(2,1)} %param.6) | data formatting | bytes 24379392 | tf_op args[1]
  18.5 6.3 reduce_max.30
  24.9 7.4 %reduce_max.28 = bf16[384]{0:T(512)(128)(2,1)S(1)} reduce(bf16[384,18944]{1,0:T(8,128)(2,1)} %param.5, bf16[]{:T(256)} %constant.47.clone.1), dimensions={1}, to_apply=%region_4.0 | reduce | flops 7274112 | bytes 14549762 | tf_op jit(solution)/shard_map/reduce_max | solution.py:15
  32.3 19.8 %copy.28 = bf16[384,18944]{0,1:T(8,128)(2,1)} copy(bf16[384,18944]{1,0:T(8,128)(2,1)} %param.5) | data formatting | bytes 29097984 | tf_op args[0]
  52.0 6.3 convert_reduce_fusion
  60.0 6.8 reduce-window.6
  67.3 15.2 %all-reduce.2 = (f32[384]{0:T(512)S(1)}, f32[384]{0:T(512)S(1)}) all-reduce(bf16[384]{0:T(512)(128)(2,1)S(1)} %reduce_max.28, bf16[384]{0:T(512)(128)(2,1)S(1)} %reduce_max.30), channel_id=1, replica_groups=mesh['dp'=4,'vocab'=8] {'vocab'}, use_global_device_ids=true, to_apply=%region_5.6 | all-reduce | flops 768 | bytes 4608 | tf_op jit(solution)/shard_map/pmax | solution.py:15
  82.5 9.2 %exponential_reduce_fusion = f32[384]{0:T(512)S(1)} fusion(bf16[384,15872]{0,1:T(8,128)(2,1)} %copy.35, f32[384]{0:T(512)S(1)} %get-tuple-element.5), kind=kLoop, calls=%fused_computation.12 | loop fusion | flops 18284160 | bytes 12192768 | tf_op jit(solution)/shard_map/reduce_sum | solution.py:22
  91.6 7.3 %fusion.2 = f32[384]{0:T(512)S(1)} fusion(bf16[384,18944]{0,1:T(8,128)(2,1)} %copy.28, f32[384]{0:T(512)S(1)} %get-tuple-element.4), kind=kLoop, calls=%fused_computation.4 | loop fusion | flops 21823104 | bytes 14552064 | tf_op jit(solution)/shard_map/reduce_sum | solution.py:16
  98.9 12.0 %all-reduce.1 = (f32[384]{0:T(512)S(1)}, f32[384]{0:T(512)S(1)}) all-reduce(f32[384]{0:T(512)S(1)} %fusion.2, f32[384]{0:T(512)S(1)} %exponential_reduce_fusion), channel_id=1, replica_groups=mesh['dp'=4,'vocab'=8] {'vocab'}, use_global_device_ids=true, to_apply=%region_7.8 | all-reduce | flops 768 | bytes 6144 | tf_op jit(solution)/shard_map/psum | solution.py:16
  110.9 15.4 %divide_convert_fusion = bf16[384,18944]{0,1:T(8,128)(2,1)} fusion(bf16[384,18944]{0,1:T(8,128)(2,1)} %copy.28, f32[384]{0:T(512)S(1)} %get-tuple-element.2, f32[384]{0:T(512)S(1)} %get-tuple-element.4), kind=kLoop, calls=%fused_computation.2 | loop fusion | flops 29097984 | bytes 29101056 | tf_op jit(solution)/shard_map/convert_element_type | solution.py:46
  126.3 19.9 %convolution_convert_fusion = bf16[148,2,128,384]{3,2,1,0:T(8,128)(2,1)} fusion(bf16[384,148,128,1]{0,2,3,1:T(8,128)(2,1)} %bitcast.47, bf16[148,2,128,128]{3,2,1,0:T(8,128)(2,1)} %param.8, f32[148,128]{1,0:T(8,128)S(1)} %convert_reduce_fusion), kind=kOutput, calls=%fused_computation.17 | convolution fusion | flops 3753639936 | bytes 53422080 | tf_op jit(solution)/shard_map/tbc,bkcd->bktd/dot_general | solution.py:69
  146.2 37.2 %copy.31 = bf16[296,384,128]{2,0,1:T(8,128)(2,1)} copy(bf16[296,384,128]{1,2,0:T(8,128)(2,1)} %bitcast.46) | data formatting | bytes 58195968 | tf_op jit(solution)/shard_map/reshape | solution.py:72
  183.4 30.6 %convolution_convert_fusion.1 = bf16[296,384,128]{2,0,1:T(8,128)(2,1)} fusion(bf16[296,384,128]{2,0,1:T(8,128)(2,1)} %copy.31, s32[296]{0:T(512)S(1)} %add_reduce_fusion), kind=kOutput, calls=%fused_computation.18 | convolution fusion | flops 8627640320 | bytes 58197152 | tf_op jit(solution)/shard_map/si,itd->std/dot_general | solution.py:73
  214.0 49.5 %copy.32 = bf16[296,384,128]{2,1,0:T(8,128)(2,1)} copy(bf16[296,384,128]{2,0,1:T(8,128)(2,1)} %convolution_convert_fusion.1) | data formatting | bytes 58195968 | tf_op jit(solution)/shard_map/convert_element_type | solution.py:76
  263.5 6.9 %all-to-all-start = ((bf16[8,37,384,128]{3,2,1,0:T(8,128)(2,1)}), bf16[8,37,384,128]{3,2,1,0:T(8,128)(2,1)}, u32[]{:S(2)}, u32[]{:S(2)}) async-start(bf16[8,37,384,128]{3,2,1,0:T(8,128)(2,1)} %bitcast.45), calls=%async_computation | async-start | bytes 58195968 | tf_op jit(solution)/shard_map/all_to_all | solution.py:77
  270.5 315.7 %all-to-all-done = bf16[8,37,384,128]{3,2,1,0:T(8,128)(2,1)} async-done(((bf16[8,37,384,128]{3,2,1,0:T(8,128)(2,1)}), bf16[8,37,384,128]{3,2,1,0:T(8,128)(2,1)}, u32[]{:S(2)}, u32[]{:S(2)}) %all-to-all-start) | async-done | bytes 29098016 | tf_op jit(solution)/shard_map/all_to_all | solution.py:77
  586.2 36.8 %fusion.4 = f32[384,124,128]{2,1,0:T(8,128)} fusion(bf16[8,37,384,128]{3,2,1,0:T(8,128)(2,1)} %all-to-all-done, s32[8,296]{1,0:T(8,128)S(1)} %add_select_fusion, s32[8,296]{1,0:T(8,128)S(1)} %fusion.27, pred[8,296]{1,0:T(8,128)(4,1)S(1)} %get-tuple-element.10), kind=kOutput, calls=%fused_computation.7 | convolution fusion | flops 3642574080 | bytes 53498688 | tf_op jit(solution)/shard_map/snd,sj->njd/dot_general | solution.py:80
  623.0 24.5 %copy.34 = f32[384,124,128]{0,2,1:T(8,128)} copy(f32[384,124,128]{2,1,0:T(8,128)} %fusion.4) | data formatting | bytes 48758784 | tf_op jit(solution)/shard_map/add | solution.py:82
  647.5 13.9 %fusion.6 = f32[384]{0:T(512)S(1)} fusion(f32[384,124,128]{0,2,1:T(8,128)} %copy.34, bf16[384,15872]{0,1:T(8,128)(2,1)} %copy.35, f32[384]{0:T(512)S(1)} %log.7, f32[384]{0:T(512)S(1)} %get-tuple-element.5), kind=kLoop, calls=%fused_computation.11 | loop fusion | flops 36568704 | bytes 36573696 | tf_op jit(solution)/shard_map/reduce_sum | solution.py:86
  661.4 11.8 %psum.37 = f32[384]{0:T(512)S(1)} all-reduce(f32[384]{0:T(512)S(1)} %fusion.6), channel_id=1, replica_groups=mesh['dp'=4,'vocab'=8] {'vocab'}, use_global_device_ids=true, to_apply=%region_13.14 | all-reduce | flops 384 | bytes 3072 | tf_op jit(solution)/shard_map/psum | solution.py:87
  673.2 1.3 fusion.30
  674.5 12.6 %all-reduce.3 = (f32[]{:T(128)}, f32[]{:T(128)}) all-reduce(f32[]{:T(128)} %get-tuple-element.8, f32[]{:T(128)} %get-tuple-element.14), channel_id=1, replica_groups=mesh['dp'=4,'vocab'=8] {'dp'}, use_global_device_ids=true, to_apply=%region_15.16 | all-reduce | flops 2 | bytes 16 | tf_op jit(solution)/shard_map/psum | solution.py:90
  (22 shorter events, 2.8 us)
Async XLA Ops:
  263.5 322.7 %all-to-all-start = ((bf16[8,37,384,128]{3,2,1,0:T(8,128)(2,1)}), bf16[8,37,384,128]{3,2,1,0:T(8,128)(2,1)}, u32[]{:S(2)}, u32[]{:S(2)}) async-start(bf16[8,37,384,128]{3,2,1,0:T(8,128)(2,1)} %bitcast.45), calls=%async_computation | async-start | bytes 58195968 | tf_op jit(solution)/shard_map/all_to_all | solution.py:77
  647.5 25.7 %copy-start = (s32[384]{0:T(512)S(1)}, s32[384]{0:T(512)}, u32[]{:S(2)}) copy-start(s32[384]{0:T(512)} %param.9) | copy-start | bytes 4612
where the time goes:
time: 692 us; the launch traced here: 689 us
  waiting for transfers between devices  316 us (46%)
  local copies, waits for them, and re-layouts  149 us (22%)
  matrix products  87.3 us (13%)
  other arithmetic  75.6 us (11%)
  blocking collectives  51.5 us (7%)
  starting transfers between devices  6.94 us (1%)
    all_to_all x1, waiting for transfers between devices, local(): lax.all_to_all(outgoing, 'vocab', split_axis=0, concat_axis=0, tiled=True)  316 us
    convert_element_type x1, local copies, waits for them, and re-layouts, local(): outgoing.astype(jnp.bfloat16).reshape(group_size, capacity, tok_rows, BLOCK)  49.5 us
    reshape x1, local copies, waits for them, and re-layouts, local(): partial_value.astype(jnp.bfloat16).reshape(tile_count, tok_rows, BLOCK)  37.2 us
    dot_general x1, matrix products, local(): jnp.einsum('snd,sj->njd', flat_items, slot_table, preferred_element_type=...  36.8 us
    unnamed x4, local copies, waits for them, and re-layouts  36.2 us
    dot_general x1, matrix products, local(): jnp.einsum('si,itd->std', placement, partial_value, preferred_element_typ...  30.6 us
    add x1, local copies, waits for them, and re-layouts, local(): target = (1.0 - SMOOTH) * mapped + SMOOTH / VS  24.5 us
    dot_general x1, matrix products, local(): jnp.einsum('tbc,bkcd->bktd', prob_blocks, mapping, preferred_element_type...  19.9 us
  transfers between devices with their start and end apart: 1, of which 1 were waited for; matrix products, arithmetic and copies ran while one was open for 0% of the time, Pallas kernels for 0%

commit v1 on v0

v1 whole, which is shorter than its diff:
```python
import functools
import math

import jax
import jax.numpy as jnp
from jax import lax
from jax.experimental import pallas as pl
from jax.experimental.pallas import tpu as pltpu
from jax.sharding import PartitionSpec as P

BLOCK = 128
SMOOTH = 0.1
CHUNK = 96
F32 = jnp.float32
BF16 = jnp.bfloat16


def kernel(n, cap, tbd, sbd, chunk, nc, c0, sidx, sblk, rord, rblk, rsrc, keep, last, valid,
           inv_ref, t_hbm, s_hbm, w_hbm, out_ref,
           tbuf, stbuf, wbuf, prob, sbuf, rbuf0, rbuf1, st_send, st_recv, tr, scl, smx, xbuf,
           in_sem, send_sem, recv_sem, sts_sem, str_sem, credit):
    me = lax.axis_index("vocab")
    slots = n * cap
    rbuf = (rbuf0, rbuf1)
    order = list(range(2, n, 2)) + list(range(3, n, 2)) + [1]
    peers = [me ^ j for j in order]
    shape = (chunk, BLOCK)
    zeros = jnp.zeros(shape, F32)
    lane = lax.broadcasted_iota(jnp.int32, shape, 1)

    def cols(b):
        return pl.ds(pl.multiple_of(b * BLOCK, BLOCK), BLOCK)

    def load_t(c):
        return pltpu.make_async_copy(t_hbm.at[pl.ds(c * chunk, chunk)], tbuf, in_sem.at[0])

    def load_s(c):
        return pltpu.make_async_copy(s_hbm.at[pl.ds(c * chunk, chunk)], stbuf, in_sem.at[1])

    load_w = pltpu.make_async_copy(w_hbm, wbuf, in_sem.at[2])
    load_t(0).start()
    load_w.start()

    barrier = pltpu.get_barrier_semaphore()
    for d in peers:
        pl.semaphore_signal(barrier, inc=1, device_id={"vocab": d})
    pl.semaphore_wait(barrier, n - 1)

    tr[...] = jnp.zeros_like(tr)

    def tile_copy(par, d):
        return pltpu.make_async_remote_copy(
            src_ref=sbuf.at[par, d], dst_ref=rbuf[par].at[pl.ds(me * cap, cap)],
            send_sem=send_sem.at[par, d], recv_sem=recv_sem.at[par, me],
            device_id={"vocab": d})

    def tile_wait(par, src):
        return pltpu.make_async_remote_copy(
            src_ref=sbuf.at[par, src], dst_ref=rbuf[par].at[pl.ds(src * cap, cap)],
            send_sem=send_sem.at[par, src], recv_sem=recv_sem.at[par, src],
            device_id={"vocab": src})

    def stat_copy(par, d):
        return pltpu.make_async_remote_copy(
            src_ref=st_send.at[par], dst_ref=st_recv.at[par, me],
            send_sem=sts_sem.at[par, d], recv_sem=str_sem.at[par, me],
            device_id={"vocab": d})

    def stat_wait(par, src):
        return pltpu.make_async_remote_copy(
            src_ref=st_send.at[par], dst_ref=st_recv.at[par, src],
            send_sem=sts_sem.at[par, src], recv_sem=str_sem.at[par, src],
            device_id={"vocab": src})

    def bcast(column):
        return jnp.broadcast_to(column, shape)

    def produce(c):
        par = c % 2
        load_t(c).wait()
        tmax = lax.fori_loop(
            0, tbd, lambda b, m: jnp.maximum(m, tbuf[:, cols(b)].astype(F32)),
            jnp.full(shape, -jnp.inf, F32), unroll=2)
        tmax = bcast(jnp.max(tmax, axis=1, keepdims=True))

        def expo(b, total):
            e = jnp.exp(tbuf[:, cols(b)].astype(F32) - tmax)
            prob[b] = (e * inv_ref[pl.ds(b, 1), :]).astype(BF16)
            return total + e

        total = lax.fori_loop(0, tbd, expo, zeros, unroll=2)
        if c + 1 < nc:
            load_t(c + 1).start()
        tsum = bcast(jnp.sum(total, axis=1, keepdims=True))
        stat = jnp.where(lane == 0, tmax, jnp.where(lane == 1, tsum, 0.0))
        if chunk < BLOCK:
            stat = jnp.concatenate([stat, jnp.zeros((BLOCK - chunk, BLOCK), F32)], axis=0)
        if c >= 2:
            for d in peers:
                stat_copy(par, d).wait_send()
        rows = stat.T[:8]
        st_send[par] = rows
        st_recv[par, me] = rows
        if c == 0:
            load_w.wait()

        def compute(d, dst):
            def one(r, carry):
                i = sidx[d * cap + r]
                b = sblk[d * cap + r]
                dst[r] = jnp.dot(prob[b], wbuf[i], preferred_element_type=F32).astype(BF16)
                return carry
            lax.fori_loop(0, cap, one, 0, unroll=4)

        for d in peers:
            if c >= 2:
                tile_copy(par, d).wait_send()
            compute(d, sbuf.at[par, d])
            if c >= 2:
                pl.semaphore_wait(credit.at[d], 1)
            stat_copy(par, d).start()
            tile_copy(par, d).start()
        compute(me, rbuf[par].at[pl.ds(me * cap, cap)])

    def student(c):
        load_s(c).wait()
        m = lax.fori_loop(
            0, sbd, lambda b, m: jnp.maximum(m, stbuf[:, cols(b)].astype(F32)),
            jnp.full(shape, -jnp.inf, F32), unroll=2)
        m = bcast(jnp.max(m, axis=1, keepdims=True))
        smx[...] = m

        def step(b, carry):
            total, lin = carry
            x = stbuf[:, cols(b)].astype(F32) - m
            xbuf[b] = x
            return total + jnp.exp(x), lin + x

        total, lin = lax.fori_loop(0, sbd, step, (zeros, zeros), unroll=2)
        if c + 1 < nc:
            load_s(c + 1).start()
        return (jnp.sum(total, axis=1, keepdims=True), jnp.sum(lin, axis=1, keepdims=True))

    def consume(c):
        par = c % 2
        ssum, slin = student(c)
        for d in peers:
            stat_wait(par, d).wait_recv()
        groups = (n * 8 + BLOCK - 1) // BLOCK
        per = BLOCK // 8
        columns = []
        for g in range(groups):
            for j in range(min(per, n - g * per)):
                tr[j * 8:j * 8 + 8, :] = st_recv[par, g * per + j]
            block = tr[...].T
            for j in range(min(per, n - g * per)):
                columns.append((block[:chunk, 8 * j:8 * j + 1], block[:chunk, 8 * j + 1:8 * j + 2]))
        gmax = functools.reduce(jnp.maximum, [m for m, _ in columns])
        gsum = sum(s * jnp.exp(m - gmax) for m, s in columns)
        for j, (m, _) in enumerate(columns):
            scl[j] = bcast(jnp.exp(m - gmax) / gsum)
        for d in peers:
            tile_wait(par, d).wait_recv()
        clogc = c0 * math.log(c0)

        def step(i, carry):
            acc, mass, lin, ent = carry
            o = rord[i]
            src = rsrc[i]
            t = rbuf[par][o].astype(F32) * (scl[src] * valid[i])
            x = xbuf[rblk[i]]
            acc = acc * keep[i] + t
            tgt = (1.0 - SMOOTH) * acc + c0
            ent = ent + last[i] * (tgt * jnp.log(tgt) - clogc)
            return acc, mass + t, lin + t * x, ent

        _, mass, lin, ent = lax.fori_loop(0, slots, step, (zeros,) * 4, unroll=2)
        mass, lin, ent = [jnp.sum(v, axis=1, keepdims=True) for v in (mass, lin, ent)]
        count = sbd * BLOCK
        kla = ent + count * clogc - (1.0 - SMOOTH) * lin - c0 * slin
        tot = (1.0 - SMOOTH) * mass + count * c0
        out_ref[pl.ds(c * chunk, chunk), :] = jnp.where(
            lane == 0, kla, jnp.where(lane == 1, tot, jnp.where(lane == 2, smx[...], ssum)))
        if c + 2 < nc:
            for d in peers:
                pl.semaphore_signal(credit.at[me], inc=1, device_id={"vocab": d})

    load_s(0).start()
    for c in range(nc):
        produce(c)
        if c >= 1:
            consume(c - 1)
    consume(nc - 1)
    for c in range(max(nc - 2, 0), nc):
        for d in peers:
            stat_copy(c % 2, d).wait_send()
            tile_copy(c % 2, d).wait_send()


def tables(tile_dest, n, cap, tbd, sbd, me):
    per = tbd * tile_dest.shape[1]
    dest = tile_dest.reshape(n, per)
    owner = dest // sbd
    block = dest % sbd
    i32 = jnp.int32
    before = jnp.arange(per)[:, None] < jnp.arange(per)[None, :]
    mine = lax.dynamic_index_in_dim(owner, me, 0, keepdims=False)
    rank = jnp.sum((mine[:, None] == mine[None, :]) & before, axis=0, dtype=i32)
    slot = mine * cap + rank
    hit = slot[:, None] == jnp.arange(n * cap)[None, :]
    sidx = jnp.sum(jnp.where(hit, jnp.arange(per, dtype=i32)[:, None], 0), axis=0)
    here = owner == me
    rrank = jnp.sum(here[:, :, None] & before[None], axis=1, dtype=i32)
    rhit = here[:, :, None] & (rrank[:, :, None] == jnp.arange(cap))
    rb = jnp.sum(jnp.where(rhit, block[:, :, None] + 1, 0), axis=1).reshape(-1)
    k = n * cap
    ids = jnp.arange(k, dtype=i32)
    key = jnp.where(rb > 0, rb - 1, sbd) * k + ids
    pos = jnp.sum(key[None, :] < key[:, None], axis=1, dtype=i32)
    order = jnp.sum(jnp.where(pos[:, None] == ids[None, :], key[:, None], 0), axis=0)
    blk = order // k
    o = order % k
    valid = (blk < sbd).astype(F32)
    same = blk[1:] == blk[:-1]
    edge = jnp.zeros((1,), bool)
    keep = jnp.concatenate([edge, same]).astype(F32)
    last = (1.0 - jnp.concatenate([same, edge]).astype(F32)) * valid
    return sidx, sidx // tile_dest.shape[1], o, jnp.minimum(blk, sbd - 1), o // cap, keep, last, valid


def local(teacher_logits, student_logits, tile_dest, tile_weight, token_mask):
    n = lax.axis_size("vocab")
    ndp = lax.axis_size("dp")
    me = lax.axis_index("vocab")
    rows = teacher_logits.shape[0]
    tbd = teacher_logits.shape[1] // BLOCK
    sbd = student_logits.shape[1] // BLOCK
    k = tile_dest.shape[1]
    cap = (tbd * k + n - 1) // n
    chunk = math.gcd(rows, CHUNK)
    nc = rows // chunk
    c0 = SMOOTH / (sbd * BLOCK * n)
    tabs = tables(tile_dest, n, cap, tbd, sbd, me)
    inv = 1.0 / jnp.sum(tile_weight.astype(F32), axis=(1, 3))
    weights = tile_weight.reshape(tbd * k, BLOCK, BLOCK)
    smem = pl.BlockSpec(memory_space=pltpu.SMEM)
    anyspec = pl.BlockSpec(memory_space=pl.ANY)
    vmem = pl.BlockSpec(memory_space=pltpu.VMEM)
    dma = pltpu.SemaphoreType.DMA
    out = pl.pallas_call(
        functools.partial(kernel, n, cap, tbd, sbd, chunk, nc, c0),
        out_shape=jax.ShapeDtypeStruct((rows, BLOCK), F32),
        in_specs=[smem] * 8 + [vmem] + [anyspec] * 3,
        out_specs=vmem,
        scratch_shapes=[
            pltpu.VMEM((chunk, tbd * BLOCK), BF16),
            pltpu.VMEM((chunk, sbd * BLOCK), BF16),
            pltpu.VMEM((tbd * k, BLOCK, BLOCK), BF16),
            pltpu.VMEM((tbd, chunk, BLOCK), BF16),
            pltpu.VMEM((2, n, cap, chunk, BLOCK), BF16),
            pltpu.VMEM((n * cap, chunk, BLOCK), BF16),
            pltpu.VMEM((n * cap, chunk, BLOCK), BF16),
            pltpu.VMEM((2, 8, BLOCK), F32),
            pltpu.VMEM((2, n, 8, BLOCK), F32),
            pltpu.VMEM((BLOCK, BLOCK), F32),
            pltpu.VMEM((n, chunk, BLOCK), F32),
            pltpu.VMEM((chunk, BLOCK), F32),
            pltpu.VMEM((sbd, chunk, BLOCK), F32),
            dma((3,)), dma((2, n)), dma((2, n)), dma((2, n)), dma((2, n)),
            pltpu.SemaphoreType.REGULAR((n,)),
        ],
        compiler_params=pltpu.CompilerParams(
            collective_id=0, has_side_effects=True, vmem_limit_bytes=64 * 2**20 - 65536),
    )(*tabs, inv, teacher_logits, student_logits, weights)
    packed = jnp.concatenate([out[:, :4].T, token_mask.astype(F32)[None]], axis=0)
    every = lax.all_gather(packed, ("dp", "vocab")).reshape(ndp, n, 5, rows)
    kla, tot, smax, ssum, mask = [every[:, :, i] for i in range(5)]
    gmax = jnp.max(smax, axis=1)
    lse = gmax + jnp.log(jnp.sum(ssum * jnp.exp(smax - gmax[:, None]), axis=1))
    token_kl = jnp.sum(kla + tot * (lse[:, None] - smax), axis=1)
    mask = mask[:, 0]
    token_loss = mask * token_kl
    mine = lax.dynamic_index_in_dim(token_loss, lax.axis_index("dp"), 0, keepdims=False)
    return mine, jnp.sum(token_loss) / jnp.sum(mask)


def solution(mesh):
    in_specs = (P("dp", "vocab"), P("dp", "vocab"), P(), P("vocab", None, None, None), P("dp"))
    out_specs = (P("dp"), P())
    return jax.shard_map(local, mesh=mesh, in_specs=in_specs, out_specs=out_specs, check_vma=False)
```

time: 692 us -> 401 us (0.58)
  Pallas kernels: 0 us -> 337 us
  waiting for transfers between devices: 316 us -> 0 us
  local copies, waits for them, and re-layouts: 149 us -> 3.38 us
  matrix products: 87.3 us -> 0 us
  other arithmetic: 75.6 us -> 15.6 us
  blocking collectives: 51.5 us -> 42.1 us
  starting transfers between devices: 6.94 us -> 0 us
    pallas_call x0 -> x1, Pallas kernels: none -> 337 us  [local(): pl.pallas_call(functools.partial(kernel, n, cap, tbd, sbd, chunk, nc, c0)...]
    all_to_all x1 -> x0, waiting for transfers between devices: 316 us -> none  [local(): lax.all_to_all(outgoing, 'vocab', split_axis=0, concat_axis=0, tiled=True)]
    dot_general x3 -> x0, matrix products: 87.3 us -> none  [the longest x1 36.8 us: local(): jnp.einsum('snd,sj->njd', flat_items, slot_table, preferred_element_type=...]
    convert_element_type x1 -> x0, local copies, waits for them, and re-layouts: 49.5 us -> none  [local(): outgoing.astype(jnp.bfloat16).reshape(group_size, capacity, tok_rows, BLOCK)]
    all_gather x0 -> x1, blocking collectives: none -> 42.1 us  [local(): every = lax.all_gather(packed, ('dp', 'vocab')).reshape(ndp, n, 5, rows)]
    reshape x1 -> x0, local copies, waits for them, and re-layouts: 37.2 us -> none  [local(): partial_value.astype(jnp.bfloat16).reshape(tile_count, tok_rows, BLOCK)]
    psum x3 -> x0, blocking collectives: 36.4 us -> none  [the longest x1 12.6 us: local(): lax.psum((jnp.sum(token_loss), jnp.sum(mask_vals)), 'dp')]
    unnamed x4 -> x2, local copies, waits for them, and re-layouts: 36.2 us -> 0.01 us
  transfers between devices with their start and end apart: 1 -> 0, of which waited for: 1 -> 0; matrix products, arithmetic and copies ran while one was open for 0% -> 0% of each run, Pallas kernels for 0% -> 0%
where the time goes in v1:
time: 401 us
  Pallas kernels  337 us (84%)
  blocking collectives  42.1 us (10%)
  other arithmetic  15.6 us (4%)
    pallas_call x1, Pallas kernels, local(): pl.pallas_call(functools.partial(kernel, n, cap, tbd, sbd, chunk, nc, c0)...  337 us
    all_gather x1, blocking collectives, local(): every = lax.all_gather(packed, ('dp', 'vocab')).reshape(ndp, n, 5, rows)  42.1 us

profile of v1, /device:TPU:0, one launch (start us, length us, event | category | flops | bytes accessed | tf_op | source)
XLA Modules:
  0.0 400.8 jit_solution(17140315386230429057)
XLA Ops:
  0.6 0.7 broadcast_remainder_fusion
  1.4 0.2 copy.36
  1.6 0.2 rem.54
  1.8 0.3 copy.37
  2.3 0.7 sign_compare_fusion
  3.0 0.3 copy.35
  3.4 0.2 ne.80
  3.7 0.5 convert_reduce_fusion.1
  4.2 0.7 select_reduce_fusion.1
  5.1 0.2 convert_reduce_fusion.2
  5.5 0.6 fusion.13
  6.2 0.7 subtract_select_fusion.last
  7.2 0.6 add_select_fusion.2
  7.8 0.6 add_convert_fusion.keep
  8.4 0.6 broadcast_minimum_fusion.rblk
  9.0 6.3 %convert_reduce_fusion = f32[148,128]{1,0:T(8,128)S(1)} fusion(bf16[148,2,128,128]{3,2,1,0:T(8,128)(2,1)} %param.8), kind=kLoop, calls=%fused_computation | loop fusion | flops 9680384 | bytes 9775104 | tf_op jit(solution)/shard_map/reduce_sum | solution.py:244
  15.3 0.7 broadcast_divide_fusion.inv_ref
  16.0 336.5 %shard_map.68 = f32[384,128]{1,0:T(8,128)} custom-call(s32[296]{0:T(512)} %copy-done, s32[296]{0:T(512)} %get-tuple-element.17.sblk, s32[296]{0:T(512)} %get-tuple-element.16.rord, s32[296]{0:T(512)} %broadcast_minimum_fusion.rblk, s32[296]{0:T(512)} %get-tuple-element.15.rsrc, f32[296]{0:T(512)} %add_convert_fusion.keep, f32[296]{0:T(512)} %subtract_select_fusion.last, ...), custom_call_target="tpu_custom_call" | custom-call | tf_op jit(solution)/shard_map/pallas_call | solution.py:250
  352.5 0.9 slice_bitcast_fusion
  353.5 0.7 convert_element_type.31
  354.3 42.1 %all-gather.1 = f32[32,5,384]{2,1,0:T(8,128)S(1)} all-gather(f32[1,5,384]{2,1,0:T(8,128)S(1)} %maximum_bitcast_fusion), channel_id=2, replica_groups=mesh['dp'=4,'vocab'=8] {'dp','vocab'}, dimensions={0}, use_global_device_ids=true | all-gather | bytes 253440 | tf_op jit(solution)/shard_map/all_gather | solution.py:276
  396.6 0.6 slice_reduce_fusion.1
  397.2 0.6 fusion.12
  399.1 0.6 dynamic-slice_reduce_fusion
  (24 shorter events, 1.2 us)
Async XLA Ops:
  7.2 1.9 copy-start
